TPU v7x, 32 devices: a whole 2x2x4 slice. The times are simulated.
32 devices in a mesh: blk: 4 (over y, x), grp: 8 (over z, core).
Axes of the slice: x: 2, y: 2, z: 4, core: 2. Of those that a mesh axis runs over, the one named last changes fastest.
Arguments:
- points: float32 [3, 4096], P(None, ('blk', 'grp')), may hold values from 0 to 1
- labels: int32 [4096], P(('blk', 'grp')), may hold values 0 or 1
- shape_scale: float32 [4096], P(('blk', 'grp')), may hold values from 0.1 to 0.4
- krylov_basis: float32 [8, 32, 4096], P(None, None, ('blk', 'grp')), may hold values from -6 to 6
- sketch: float32 [1024, 4096], P(None, ('blk', 'grp')), may hold values from -0.09375 to 0.09375
- sketched_basis: float32 [8, 32, 1024], replicated, may hold values from -0.1875 to 0.1875
Outputs:
- next_vector: float32 [32, 4096], P(None, ('blk', 'grp'))
- coefficients: float32 [8, 32], replicated
- sketch_next: float32 [32, 1024], replicated
- norms: float32 [32], replicated
All inputs are finite; a program needn't handle non-finite values. No bound on the sum of `labels` on one device may be relied on, other than what follows from the above.
Results may differ from a plain program's by a relative error of at most 0.0003.
Values sent between devices are 32-bit elements; how exact they have to be, the bound alone decides.
A program may use at most 64 MiB of HBM per device.

v0:
```python
import math
import jax
import jax.numpy as jnp
from jax import lax
from jax.sharding import PartitionSpec as P

SYSTEMS = 32
KRYLOV = 8


def kernel_terms(target_points, target_labels, source_block):
    source_points = source_block[0:3]
    scales = source_block[3]
    weights_block = source_block[4:]
    delta_x = source_points[0][:, None] - target_points[0][None, :]
    delta_y = source_points[1][:, None] - target_points[1][None, :]
    delta_z = source_points[2][:, None] - target_points[2][None, :]
    radius_sq = delta_x * delta_x + delta_y * delta_y + delta_z * delta_z
    squared_scale = (scales * scales)[:, None]
    shifted = radius_sq + squared_scale
    inverse = lax.rsqrt(shifted)
    boundary = shifted * inverse
    interior = (3.0 * squared_scale + 2.0 * radius_sq) * inverse * inverse * inverse
    kernel = jnp.where(target_labels[None, :] == 1, interior, boundary)
    return jnp.dot(
        weights_block, kernel, precision=lax.Precision.HIGHEST, preferred_element_type=jnp.float32
    )


def block_size(length, wanted):
    return wanted if length % wanted == 0 else length


def accumulate(running, target_points, target_labels, source_block):
    target_count = target_points.shape[1]
    source_count = source_block.shape[1]
    tblock = block_size(target_count, 2048)
    sblock = block_size(source_count, 2048)
    system_rows = running.shape[0]

    def over_targets(target_index, current):

        def over_sources(source_index, partial_value):
            portion = lax.dynamic_slice_in_dim(source_block, source_index * sblock, sblock, 1)
            return partial_value + kernel_terms(target_points, target_labels, portion)

        partial_value = lax.fori_loop(
            0, source_count // sblock, over_sources, jnp.zeros((system_rows, tblock), jnp.float32)
        )
        return current + partial_value

    return lax.fori_loop(0, target_count // tblock, over_targets, running)


def shards(points, labels, shape_scale, krylov_basis, sketch, sketched_basis):
    own_count = points.shape[1]
    everything = lax.axis_size("blk") * lax.axis_size("grp") * own_count
    sources = jnp.concatenate([points, shape_scale[None, :], krylov_basis[KRYLOV - 1]], axis=0)
    empty = jnp.zeros((SYSTEMS, own_count), jnp.float32)
    summed = accumulate(
        empty, points, labels, lax.all_gather(sources, ("blk", "grp"), axis=1, tiled=True)
    )
    image = summed / math.sqrt(everything)
    local_sketch = lax.dot_general(
        image,
        sketch,
        (((1,), (1,)), ((), ())),
        precision=lax.Precision.HIGHEST,
        preferred_element_type=jnp.float32,
    )
    sketched = lax.psum(local_sketch, ("blk", "grp"))
    coefficients = jnp.einsum(
        "jrk,rk->jr", sketched_basis, sketched, precision=lax.Precision.HIGHEST
    )
    remainder = sketched - jnp.einsum(
        "jr,jrk->rk", coefficients, sketched_basis, precision=lax.Precision.HIGHEST
    )
    norms = jnp.sqrt(jnp.mean(remainder * remainder, axis=1) + 1e-06)
    sketch_next = remainder / norms[:, None]
    reduced = image - jnp.einsum(
        "jr,jrn->rn", coefficients, krylov_basis, precision=lax.Precision.HIGHEST
    )
    next_vector = reduced / norms[:, None]
    return (next_vector, coefficients, sketch_next, norms)


def solution(mesh):
    placed = (
        P(None, ("blk", "grp")),
        P(("blk", "grp")),
        P(("blk", "grp")),
        P(None, None, ("blk", "grp")),
        P(None, ("blk", "grp")),
        P(),
    )
    return jax.shard_map(
        shards,
        mesh=mesh,
        in_specs=placed,
        out_specs=(P(None, ("blk", "grp")), P(), P(), P()),
        check_vma=False,
    )
```

profile of v0, /device:TPU:0, one launch (start us, length us, event | category | flops | bytes accessed | tf_op | source)
XLA Modules:
  0.0 195.9 jit_solution(17373773227067051160)
XLA Ops:
  7.2 0.0 copy-start
  7.2 0.0 all-reduce.2.cloned.1.call-start
  7.2 0.0 copy-start.4
  7.2 0.8 slice_bitcast_fusion.3
  8.0 0.0 copy-start.7
  8.1 0.0 copy-done.4
  8.1 0.7 copy-done.7
  8.7 0.0 copy-start.8
  8.7 45.9 %all_gather.3 = f32[36,4096]{1,0:T(8,128)S(1)} all-gather(f32[36,128]{1,0:T(8,128)S(1)} %pad_maximum_fusion), channel_id=1, replica_groups=mesh['blk'=4,'grp'=8] {'blk','grp'}, dimensions={1}, use_global_device_ids=true | all-gather | bytes 608256 | tf_op jit(solution)/shard_map/all_gather | solution.py:61
  54.7 0.0 copy-done.8
  54.7 0.0 copy-start.2
  54.7 4.4 %while.21 = (s32[]{:T(128)}, f32[32,128]{1,0:T(8,128)S(1)}, f32[36,4096]{1,0:T(8,128)S(1)}, s32[128]{0:T(128)S(1)}, f32[3,128]{1,0:T(4,128)S(1)}, /*index=5*/s32...) while((s32[]{:T(128)}, f32[32,128]{1,0:T(8,128)S(1)}, ...), condition=%wide.region_1.0_spmd.clone, body=%wide.region_0.1_spmd.clone.sunk | while | flops 104870024 | bytes 423813 | solution.py:47
  54.7 0.1 constant_dynamic-slice_fusion.2
  54.8 2.0 %convolution_add_fusion.2 = f32[32,128]{1,0:T(8,128)S(1)} fusion(f32[2048]{0:T(1024)S(1)} %bitcast.42, f32[128]{0:T(128)S(1)} %get-tuple-element.195, f32[2048]{0:T(1024)S(1)} %bitcast.45, f32[128]{0:T(128)S(1)} %get-tuple-element.197, f32[2048]{0:T(1024)S(1)} %bitcast.44, f32[128]{0:T(128)S(1)} %get-tuple-element.199, f32[2048]{0:T(1024)S(1)} %bitcast.43, ...), kind=kOutput, calls=%fused_computation.2.clone.1 | convolution fusion | flops 104865792 | bytes 337929 | tf_op jit(solution)/shard_map/while/body/eval_jaxpr/while/body/eval_jaxpr/dot_general | solution.py:25
  56.9 0.1 constant_dynamic-slice_fusion.2
  57.0 2.0 %convolution_add_fusion.2 = f32[32,128]{1,0:T(8,128)S(1)} fusion(f32[2048]{0:T(1024)S(1)} %bitcast.42, f32[128]{0:T(128)S(1)} %get-tuple-element.195, f32[2048]{0:T(1024)S(1)} %bitcast.45, f32[128]{0:T(128)S(1)} %get-tuple-element.197, f32[2048]{0:T(1024)S(1)} %bitcast.44, f32[128]{0:T(128)S(1)} %get-tuple-element.199, f32[2048]{0:T(1024)S(1)} %bitcast.43, ...), kind=kOutput, calls=%fused_computation.2.clone.1 | convolution fusion | flops 104865792 | bytes 337929 | tf_op jit(solution)/shard_map/while/body/eval_jaxpr/while/body/eval_jaxpr/dot_general | solution.py:25
  59.1 0.0 copy-done.2
  59.1 1.3 fusion.32
  60.3 0.0 all-reduce.2.cloned.1.call-update
  60.4 120.9 %all-reduce.2.cloned.1.call-done = f32[32,1024]{1,0:T(8,128)} async-done(((f32[32,1024]{1,0:T(8,128)}), f32[32,1024]{1,0:T(8,128)}) %all-reduce.2.cloned.1.call-update) | async-done | bytes 131088 | tf_op jit(solution)/shard_map/psum | solution.py:71
  181.2 0.0 copy-done
  181.2 0.0 copy-start.3
  181.3 3.6 %fusion.27 = f32[32,1,8]{2,1,0:T(1,128)S(1)} fusion(f32[8,32,1024]{2,1,0:T(8,128)S(1)} %copy-done, f32[32,1024,1]{1,0,2:T(8,128)} %bitcast.40), kind=kOutput, calls=%fused_computation.36 | convolution fusion | flops 3145728 | bytes 1180672 | tf_op jit(solution)/shard_map/jrk,rk->jr/dot_general | solution.py:72
  184.8 0.1 copy.12
  184.9 0.0 copy-start.5
  184.9 0.1 copy.13
  185.0 0.5 copy-done.5
  185.5 0.0 copy-done.3
  185.5 0.4 fusion.29
  185.9 0.0 copy-start.1
  185.9 1.5 fusion.25
  187.4 0.0 copy-done.1
  187.4 0.1 multiply_reduce_fusion
  187.6 0.0 copy-start.6
  187.6 0.7 subtract_divide_fusion
  188.3 0.0 copy-done.6
  188.3 0.7 broadcast_divide_fusion
  (9 shorter events, 0.0 us)
Async XLA Ops:
  7.2 174.1 %copy-start = (f32[8,32,1024]{2,1,0:T(8,128)S(1)}, f32[8,32,1024]{2,1,0:T(8,128)}, u32[]{:S(2)}) copy-start(f32[8,32,1024]{2,1,0:T(8,128)} %param.13) | copy-start | bytes 3145732
  7.2 174.1 %all-reduce.2.cloned.1.call-start = ((), (), s32[]{:S(2)}) async-start(), calls=%async_computation | async-start | bytes 262144 | tf_op jit(solution)/shard_map/psum | solution.py:71
  7.2 0.8 copy-start.4
  8.0 0.7 copy-start.7
  8.7 46.0 %copy-start.8 = (s32[128]{0:T(128)S(1)}, s32[128]{0:T(128)}, u32[]{:S(2)}) copy-start(s32[128]{0:T(128)} %param.9) | copy-start | bytes 1540
  54.7 4.4 %copy-start.2 = (f32[1024,128]{1,0:T(8,128)S(1)}, f32[1024,128]{1,0:T(8,128)}, u32[]{:S(2)}) copy-start(f32[1024,128]{1,0:T(8,128)} %param.12) | copy-start | bytes 1572868
  181.2 4.3 %copy-start.3 = (f32[8,32,128]{2,1,0:T(8,128)S(1)}, f32[8,32,128]{2,1,0:T(8,128)}, u32[]{:S(2)}) copy-start(f32[8,32,128]{2,1,0:T(8,128)} %param.11) | copy-start | bytes 393220
  184.9 0.6 copy-start.5
  185.9 1.5 copy-start.1
  187.6 0.7 copy-start.6
Sparse Core Ops, SparseCore 0:
  60.5 120.7 all-reduce.1
where the time goes:
time: 196 us
  waiting for transfers between devices  121 us (62%)
  blocking collectives  45.9 us (23%)
  between operations  14.1 us (7%)
  matrix products  10.7 us (5%)
  local copies, waits for them, and re-layouts  2.17 us (1%)
    psum x1, waiting for transfers between devices, shards(): sketched = lax.psum(local_sketch, ('blk', 'grp'))  121 us
    all_gather x1, blocking collectives, shards(): lax.all_gather(sources, ('blk', 'grp'), axis=1, tiled=True)  45.9 us
    dot_general x2, matrix products, kernel_terms(): jnp.dot(weights_block, kernel, precision=lax.Precision.HIGHEST, preferred...  4 us
  transfers between devices with their start and end apart: 1, of which 1 were waited for; matrix products, arithmetic and copies ran while one was open for 0% of the time, Pallas kernels for 0%

commit v1 on v0

--- a/solution.py
+++ b/solution.py
@@ -68,7 +68,7 @@
         precision=lax.Precision.HIGHEST,
         preferred_element_type=jnp.float32,
     )
-    sketched = lax.psum(local_sketch, ("blk", "grp"))
+    sketched = jnp.sum(lax.all_gather(local_sketch, ("blk", "grp")), axis=0)
     coefficients = jnp.einsum(
         "jrk,rk->jr", sketched_basis, sketched, precision=lax.Precision.HIGHEST
     )

time: 196 us -> 137 us (0.70)
  waiting for transfers between devices: 121 us -> 58.1 us
  other arithmetic: 1.87 us -> 6.34 us
    psum x1 -> x0, waiting for transfers between devices: 121 us -> none  [shards(): sketched = lax.psum(local_sketch, ('blk', 'grp'))]
    all_gather x0 -> x1, waiting for transfers between devices: none -> 58.1 us  [shards(): sketched = jnp.sum(lax.all_gather(local_sketch, ('blk', 'grp')), axis=0)]
    reduce_sum x0 -> x1, other arithmetic: none -> 2.43 us  [shards(): sketched = jnp.sum(lax.all_gather(local_sketch, ('blk', 'grp')), axis=0)]
where the time goes in v1:
time: 137 us
  waiting for transfers between devices  58.1 us (42%)
  blocking collectives  45.9 us (34%)
  between operations  14.1 us (10%)
  matrix products  9.92 us (7%)
  other arithmetic  6.34 us (5%)
  local copies, waits for them, and re-layouts  2.56 us (2%)
    all_gather x1, waiting for transfers between devices, shards(): sketched = jnp.sum(lax.all_gather(local_sketch, ('blk', 'grp')), axis=0)  58.1 us
    all_gather x1, blocking collectives, shards(): lax.all_gather(sources, ('blk', 'grp'), axis=1, tiled=True)  45.9 us
    dot_general x2, matrix products, kernel_terms(): jnp.dot(weights_block, kernel, precision=lax.Precision.HIGHEST, preferred...  4 us
    dot_general x1, matrix products, shards(): jnp.einsum('jrk,rk->jr', sketched_basis, sketched, precision=lax.Precisio...  2.74 us
  transfers between devices with their start and end apart: 1, of which 1 were waited for; matrix products, arithmetic and copies ran while one was open for 0% of the time, Pallas kernels for 0%

profile of v1, /device:TPU:0, one launch (start us, length us, event | category | flops | bytes accessed | tf_op | source)
XLA Modules:
  0.0 137.0 jit_solution(6235236021583655064)
XLA Ops:
  7.2 0.0 copy-start
  7.2 0.0 all-gather.3.cloned.1.call-start
  7.2 0.8 slice_bitcast_fusion.3
  8.0 0.7 pad_maximum_fusion
  8.7 45.9 %all_gather.9 = f32[36,4096]{1,0:T(8,128)S(1)} all-gather(f32[36,128]{1,0:T(8,128)S(1)} %pad_maximum_fusion), channel_id=1, replica_groups=mesh['blk'=4,'grp'=8] {'blk','grp'}, dimensions={1}, use_global_device_ids=true | all-gather | bytes 608256 | tf_op jit(solution)/shard_map/all_gather | solution.py:61
  54.7 0.0 copy-start.1
  54.7 7.3 %while.21 = (s32[]{:T(128)}, f32[32,128]{1,0:T(8,128)S(1)}, f32[36,4096]{1,0:T(8,128)S(1)}, s32[128]{0:T(128)}, f32[3,128]{1,0:T(4,128)}, /*index=5*/s32[]{:T(12...) while((s32[]{:T(128)}, f32[32,128]{1,0:T(8,128)S(1)}, ...), condition=%wide.region_1.0_spmd.clone, body=%wide.region_0.1_spmd.clone.sunk | while | flops 104870024 | bytes 423813 | solution.py:47
  54.7 0.7 broadcast_compare_fusion.2
  55.4 0.8 slice_bitcast_fusion.5
  56.2 0.1 constant_dynamic-slice_fusion.2
  56.3 2.0 %convolution_add_fusion.2 = f32[32,128]{1,0:T(8,128)S(1)} fusion(f32[2048]{0:T(1024)S(1)} %bitcast.44, f32[128]{0:T(128)S(1)} %get-tuple-element.195, f32[2048]{0:T(1024)S(1)} %bitcast.47, f32[128]{0:T(128)S(1)} %get-tuple-element.197, f32[2048]{0:T(1024)S(1)} %bitcast.46, f32[128]{0:T(128)S(1)} %get-tuple-element.199, f32[2048]{0:T(1024)S(1)} %bitcast.45, ...), kind=kOutput, calls=%fused_computation.2.clone.1 | convolution fusion | flops 104865792 | bytes 337929 | tf_op jit(solution)/shard_map/while/body/eval_jaxpr/while/body/eval_jaxpr/dot_general | solution.py:25
  58.3 0.7 broadcast_compare_fusion.2
  59.0 0.8 slice_bitcast_fusion.5
  59.8 0.1 constant_dynamic-slice_fusion.2
  59.9 2.0 %convolution_add_fusion.2 = f32[32,128]{1,0:T(8,128)S(1)} fusion(f32[2048]{0:T(1024)S(1)} %bitcast.44, f32[128]{0:T(128)S(1)} %get-tuple-element.195, f32[2048]{0:T(1024)S(1)} %bitcast.47, f32[128]{0:T(128)S(1)} %get-tuple-element.197, f32[2048]{0:T(1024)S(1)} %bitcast.46, f32[128]{0:T(128)S(1)} %get-tuple-element.199, f32[2048]{0:T(1024)S(1)} %bitcast.45, ...), kind=kOutput, calls=%fused_computation.2.clone.1 | convolution fusion | flops 104865792 | bytes 337929 | tf_op jit(solution)/shard_map/while/body/eval_jaxpr/while/body/eval_jaxpr/dot_general | solution.py:25
  62.0 0.0 copy-start.2
  62.0 0.0 copy-done.1
  62.0 1.3 fusion.32
  63.2 0.0 all-gather.3.cloned.1.call-update
  63.3 58.1 %all-gather.3.cloned.1.call-done = f32[1024,1024]{1,0:T(8,128)} async-done(((f32[32,1024]{1,0:T(8,128)}), f32[1024,1024]{1,0:T(8,128)}) %all-gather.3.cloned.1.call-update) | async-done | bytes 4194320 | tf_op jit(solution)/shard_map/all_gather | solution.py:71
  121.3 2.4 %reduce_sum.18 = f32[32,1024]{1,0:T(8,128)S(1)} reduce(f32[32,32,1024]{2,1,0:T(8,128)} %bitcast.41, f32[]{:T(128)} %constant.57.clone.1), dimensions={0}, to_apply=%region_2.0 | reduce | flops 1015808 | bytes 4325380 | tf_op jit(solution)/shard_map/reduce_sum | solution.py:71
  123.8 0.0 copy-done
  123.8 2.7 %fusion.27 = f32[32,1,8]{2,1,0:T(1,128)S(1)} fusion(f32[8,32,1024]{2,1,0:T(8,128)S(1)} %copy-done, f32[32,1024,1]{1,0,2:T(8,128)S(1)} %bitcast.42), kind=kOutput, calls=%fused_computation.36 | convolution fusion | flops 3145728 | bytes 1180672 | tf_op jit(solution)/shard_map/jrk,rk->jr/dot_general | solution.py:72
  126.5 0.1 copy.12
  126.6 0.0 copy-start.3
  126.6 0.1 copy.13
  126.7 0.0 copy-done.2
  126.7 0.4 fusion.29
  127.1 1.5 %fusion.25 = f32[32,1,1024]{2,1,0:T(1,128)S(1)} fusion(f32[8,32,1]{0,2,1:T(1,128)S(1)} %copy.13, f32[8,32,1024]{2,1,0:T(8,128)S(1)} %copy-done), kind=kOutput, calls=%fused_computation.34 | convolution fusion | flops 3145728 | bytes 1180672 | tf_op jit(solution)/shard_map/jr,jrk->rk/dot_general | solution.py:75
  128.6 0.1 multiply_reduce_fusion
  128.7 0.0 copy-start.4
  128.8 0.7 broadcast_divide_fusion
  129.5 0.7 subtract_divide_fusion
  130.2 0.0 copy-done.3
  130.2 0.0 copy-done.4
  (4 shorter events, 0.0 us)
Async XLA Ops:
  7.2 116.6 %copy-start = (f32[8,32,1024]{2,1,0:T(8,128)S(1)}, f32[8,32,1024]{2,1,0:T(8,128)}, u32[]{:S(2)}) copy-start(f32[8,32,1024]{2,1,0:T(8,128)} %param.13) | copy-start | bytes 3145732
  7.2 114.1 %all-gather.3.cloned.1.call-start = ((), (), s32[]{:S(2)}) async-start(), calls=%async_computation | async-start | bytes 4325376 | tf_op jit(solution)/shard_map/all_gather | solution.py:71
  54.7 7.3 %copy-start.1 = (f32[1024,128]{1,0:T(8,128)S(1)}, f32[1024,128]{1,0:T(8,128)}, u32[]{:S(2)}) copy-start(f32[1024,128]{1,0:T(8,128)} %param.12) | copy-start | bytes 1572868
  62.0 64.7 %copy-start.2 = (f32[8,32,128]{2,1,0:T(8,128)S(1)}, f32[8,32,128]{2,1,0:T(8,128)}, u32[]{:S(2)}) copy-start(f32[8,32,128]{2,1,0:T(8,128)} %param.11) | copy-start | bytes 393220
  126.6 3.6 %copy-start.3 = (f32[32,1,8]{0,2,1:T(8,128)}, f32[32,1,8]{0,2,1:T(8,128)S(1)}, u32[]{:S(2)}) copy-start(f32[32,1,8]{0,2,1:T(8,128)S(1)} %copy.12) | copy-start | bytes 3076
  128.7 1.4 %copy-start.4 = (f32[32]{0:T(128)}, f32[32]{0:T(128)S(1)}, u32[]{:S(2)}) copy-start(f32[32]{0:T(128)S(1)} %add_sqrt_fusion) | copy-start | bytes 388
Sparse Core Ops, SparseCore 0:
  63.4 57.9 all-gather.2
